TPU v7x, 8 devices: a whole 2x2x1 slice. The times are simulated.
8 devices in a mesh: batch: 1 (over z), row: 2 (over y), col: 4 (over x, core).
Axes of the slice: x: 2, y: 2, z: 1, core: 2. Of those that a mesh axis runs over, the one named last changes fastest.
Arguments:
- lower_tri: bfloat16 [2048, 2048], P(('batch', 'row'), 'col')
- right_side: bfloat16 [2048, 16384], P(('batch', 'row'), 'col')
- grad_out: bfloat16 [2048, 16384], P(('batch', 'row'), 'col')
Outputs:
- output 1: bfloat16 [2048, 16384], P(('batch', 'row'), 'col')
- output 2: bfloat16 [2048, 2048], P(('batch', 'row'), 'col')
All inputs are finite; a program needn't handle non-finite values.
Results may differ from a plain program's by a relative error of at most 0.001.
Values are sent between devices in bfloat16 or wider.
A program may use at most 1 GiB of HBM per device.

v0:
```python
import jax
import jax.numpy as jnp
from jax import lax
from jax.sharding import PartitionSpec as P

BLOCK_SIZE = 256


def solution(mesh):
    mesh_rows = mesh.shape["row"]
    mesh_cols = mesh.shape["col"]
    group_size = max(mesh_rows, mesh_cols)
    row_step = group_size // mesh_rows
    col_step = group_size // mesh_cols
    block_spec = P(("batch", "row"), "col")

    def per_device(lower_tri, right_side, grad_out):
        rows_here, cols_here = lower_tri.shape
        num_cols = right_side.shape[1]
        num_steps = rows_here // (row_step * BLOCK_SIZE)
        right_pieces = []
        lower_pieces = []
        for step_idx in range(num_steps):
            first_row = step_idx * row_step * BLOCK_SIZE
            left_rows = rows_here - first_row
            grad_rows = grad_out[first_row:]
            lower_panel = lower_tri[first_row:, step_idx * col_step * BLOCK_SIZE:(step_idx + 1) * col_step * BLOCK_SIZE]
            gathered = lax.all_gather(lower_panel.reshape(left_rows, col_step, BLOCK_SIZE), "col", axis=2)
            right_part = jnp.einsum("rbqe,rf->bqef", gathered, grad_rows, preferred_element_type=jnp.float32)
            right_mine = lax.psum_scatter(right_part.reshape(row_step, mesh_rows * BLOCK_SIZE, num_cols), "row", scatter_dimension=1, tiled=True)
            right_pieces.append(right_mine.reshape(row_step * BLOCK_SIZE, num_cols).astype(jnp.bfloat16))
            side_block = right_side[first_row:first_row + row_step * BLOCK_SIZE].reshape(row_step, BLOCK_SIZE, num_cols)
            side_rows = lax.all_gather(side_block, "row", axis=1).reshape(col_step, mesh_cols, BLOCK_SIZE, num_cols)
            lower_part = jnp.einsum("rf,bqef->rbqe", grad_rows, side_rows, preferred_element_type=jnp.float32)
            lower_mine = lax.psum_scatter(lower_part.reshape(left_rows, col_step, mesh_cols * BLOCK_SIZE), "col", scatter_dimension=2, tiled=True)
            lower_piece = lower_mine.reshape(left_rows, col_step * BLOCK_SIZE).astype(jnp.bfloat16)
            lower_pieces.append(jnp.pad(lower_piece, ((first_row, 0), (0, 0))))
        grad_right = jnp.concatenate(right_pieces, axis=0)
        grad_lower = jnp.concatenate(lower_pieces, axis=1)
        row_pos = jnp.arange(rows_here)[:, None]
        col_pos = jnp.arange(cols_here)[None, :]
        row_global = (row_pos // BLOCK_SIZE * mesh_rows + lax.axis_index("row")) * BLOCK_SIZE + row_pos % BLOCK_SIZE
        col_global = (col_pos // BLOCK_SIZE * mesh_cols + lax.axis_index("col")) * BLOCK_SIZE + col_pos % BLOCK_SIZE
        grad_lower = jnp.where(row_global >= col_global, grad_lower, 0.0).astype(jnp.bfloat16)
        return grad_right, grad_lower

    return jax.shard_map(per_device, mesh=mesh, in_specs=(block_spec, block_spec, block_spec), out_specs=(block_spec, block_spec), check_vma=False)
```

profile of v0, /device:TPU:1, one launch (start us, length us, event | category | flops | bytes accessed | tf_op | source)
XLA Modules:
  0.0 726.0 jit_solution(726481674572947868)
XLA Ops:
  7.2 6.1 fusion.34
  13.3 0.0 all-gather.7.cloned.1.call-start
  13.3 0.7 all-gather.7.cloned.1.call-update
  14.0 0.0 all-gather.13.cloned.1.call-start
  14.1 0.4 copy-done
  14.5 0.7 slice.16
  15.2 0.0 all-gather.11.cloned.1.call-start
  15.3 0.8 slice.15
  16.1 0.0 reduce-scatter.11.cloned.1.call-start
  16.2 101.1 %all-gather.9.cloned.1.call-done = bf16[2,2,256,4096]{3,2,1,0:T(8,128)(2,1)} async-done(((bf16[2,1,256,4096]{3,2,1,0:T(8,128)(2,1)}), bf16[2,2,256,4096]{3,2,1,0:T(8,128)(2,1)}) %all-gather.9.cloned.1.call-update) | async-done | bytes 8388624 | tf_op jit(solution)/shard_map/all_gather | solution.py:33
  117.3 10.5 %fusion.8 = f32[512,1,1024]{2,0,1:T(8,128)} fusion(bf16[1024,4096]{1,0:T(8,128)(2,1)} %bitcast.42, bf16[1024,4096]{1,0:T(8,128)(2,1)} %param.5), kind=kOutput, calls=%fused_computation.12 | convolution fusion | flops 4294967296 | bytes 14680064 | tf_op jit(solution)/shard_map/rf,bqef->rbqe/dot_general | solution.py:34
  127.8 0.0 reduce-scatter.9.cloned.1.call-start
  127.9 93.8 %all-gather.7.cloned.1.call-done = bf16[2,2,256,4096]{3,2,1,0:T(8,128)(2,1)} async-done(((bf16[2,1,256,4096]{3,2,1,0:T(8,128)(2,1)}), bf16[2,2,256,4096]{3,2,1,0:T(8,128)(2,1)}) %all-gather.7.cloned.1.call-update) | async-done | bytes 8388624 | tf_op jit(solution)/shard_map/all_gather | solution.py:33
  221.7 15.0 %convolution_bitcast_fusion = f32[1024,1,1024]{2,0,1:T(8,128)} fusion(bf16[1024,4096]{1,0:T(8,128)(2,1)} %param.5, bf16[1024,4096]{1,0:T(8,128)(2,1)} %bitcast.41), kind=kOutput, calls=%fused_computation.8 | convolution fusion | flops 8589934592 | bytes 20971520 | tf_op jit(solution)/shard_map/rf,bqef->rbqe/dot_general | solution.py:34
  236.7 0.0 reduce-scatter.7.cloned.1.call-start
  236.8 0.9 all-gather.13.cloned.1.call-done
  237.7 1.5 copy.10
  239.2 10.2 %fusion.2 = f32[2,512,4096]{2,1,0:T(8,128)} fusion(bf16[2,512,512]{2,1,0:T(8,128)(2,1)S(1)} %bitcast.40, bf16[1024,4096]{1,0:T(8,128)(2,1)} %param.5), kind=kOutput, calls=%fused_computation.3 | convolution fusion | flops 4294967296 | bytes 22020096 | tf_op jit(solution)/shard_map/rbqe,rf->bqef/dot_general | solution.py:29
  249.5 0.2 reduce-scatter.5.cloned.1.call-start
  249.7 9.8 %all-gather.11.cloned.1.call-done = bf16[1024,1024]{1,0:T(8,128)(2,1)} async-done(((bf16[1024,256]{1,0:T(8,128)(2,1)}), bf16[1024,1024]{1,0:T(8,128)(2,1)}) %all-gather.11.cloned.1.call-update) | async-done | bytes 2097168 | tf_op jit(solution)/shard_map/all_gather | solution.py:28
  259.5 2.9 copy.9
  262.4 14.5 %fusion = f32[2,512,4096]{2,1,0:T(8,128)} fusion(bf16[2,512,1024]{2,1,0:T(8,128)(2,1)S(1)} %bitcast.39, bf16[1024,4096]{1,0:T(8,128)(2,1)} %param.5), kind=kOutput, calls=%fused_computation.1 | convolution fusion | flops 8589934592 | bytes 27262976 | tf_op jit(solution)/shard_map/rbqe,rf->bqef/dot_general | solution.py:29
  276.9 9.8 %reduce-scatter.11.cloned.1.call-done = f32[512,1,256]{2,0,1:T(8,128)} async-done(((f32[512,1,1024]{2,0,1:T(8,128)}), f32[512,1,256]{2,0,1:T(8,128)}) %reduce-scatter.11.cloned.1.call-update) | async-done | bytes 524304 | tf_op jit(solution)/shard_map/reduce_scatter | solution.py:35
  286.7 1.1 convert_bitcast_fusion.1
  287.8 40.2 %reduce-scatter.9.cloned.1.call-done = f32[1024,1,256]{2,0,1:T(8,128)} async-done(((f32[1024,1,1024]{2,0,1:T(8,128)}), f32[1024,1,256]{2,0,1:T(8,128)}) %reduce-scatter.9.cloned.1.call-update) | async-done | bytes 1048592 | tf_op jit(solution)/shard_map/reduce_scatter | solution.py:35
  328.0 1.3 convert_bitcast_fusion
  329.2 1.3 compare_select_fusion
  330.5 186.1 %reduce-scatter.7.cloned.1.call-done = f32[2,256,4096]{2,1,0:T(8,128)} async-done(((f32[2,512,4096]{2,1,0:T(8,128)}), f32[2,256,4096]{2,1,0:T(8,128)}) %reduce-scatter.7.cloned.1.call-update) | async-done | bytes 8388624 | tf_op jit(solution)/shard_map/reduce_scatter | solution.py:30
  516.6 6.0 convert_element_type.30
  522.5 182.6 %reduce-scatter.5.cloned.1.call-done = f32[2,256,4096]{2,1,0:T(8,128)} async-done(((f32[2,512,4096]{2,1,0:T(8,128)}), f32[2,256,4096]{2,1,0:T(8,128)}) %reduce-scatter.5.cloned.1.call-update) | async-done | bytes 8388624 | tf_op jit(solution)/shard_map/reduce_scatter | solution.py:30
  705.2 6.0 convert_element_type.28
  711.2 8.0 %pad_maximum_fusion = bf16[1024,4096]{1,0:T(8,128)(2,1)} fusion(bf16[512,4096]{1,0:T(8,128)(2,1)} %bitcast.35, bf16[512,4096]{1,0:T(8,128)(2,1)} %bitcast.36), kind=kLoop, calls=%fused_computation | loop fusion | flops 16777216 | bytes 16777216 | tf_op jit(solution)/shard_map/concatenate | solution.py:38
  (11 shorter events, 0.2 us)
Async XLA Ops:
  7.2 110.1 %all-gather.9.cloned.1.call-start = ((), (), s32[]{:S(2)}) async-start(), calls=%async_computation.8 | async-start | bytes 12582912 | tf_op jit(solution)/shard_map/all_gather | solution.py:33
  13.3 1.2 copy-start
  13.3 208.4 %all-gather.7.cloned.1.call-start = ((), (), s32[]{:S(2)}) async-start(), calls=%async_computation.6 | async-start | bytes 12582912 | tf_op jit(solution)/shard_map/all_gather | solution.py:33
  14.0 223.7 %all-gather.13.cloned.1.call-start = ((), (), s32[]{:S(2)}) async-start(), calls=%async_computation.11 | async-start | bytes 1310720 | tf_op jit(solution)/shard_map/all_gather | solution.py:28
  15.2 244.3 %all-gather.11.cloned.1.call-start = ((), (), s32[]{:S(2)}) async-start(), calls=%async_computation.10 | async-start | bytes 2621440 | tf_op jit(solution)/shard_map/all_gather | solution.py:28
  16.1 270.6 %reduce-scatter.11.cloned.1.call-start = ((), (), s32[]{:S(2)}) async-start(), calls=%async_computation.9 | async-start | bytes 2621440 | tf_op jit(solution)/shard_map/reduce_scatter | solution.py:35
  127.8 200.2 %reduce-scatter.9.cloned.1.call-start = ((), (), s32[]{:S(2)}) async-start(), calls=%async_computation.7 | async-start | bytes 5242880 | tf_op jit(solution)/shard_map/reduce_scatter | solution.py:35
  236.7 279.9 %reduce-scatter.7.cloned.1.call-start = ((), (), s32[]{:S(2)}) async-start(), calls=%async_computation.5 | async-start | bytes 25165824 | tf_op jit(solution)/shard_map/reduce_scatter | solution.py:30
  249.5 455.7 %reduce-scatter.5.cloned.1.call-start = ((), (), s32[]{:S(2)}) async-start(), calls=%async_computation.4 | async-start | bytes 25165824 | tf_op jit(solution)/shard_map/reduce_scatter | solution.py:30
Sparse Core Ops, SparseCore 0:
  13.4 103.8 all-gather.8
  119.4 102.2 all-gather.6
  223.2 14.4 all-gather.12
  239.7 19.7 all-gather.10
  261.8 24.8 reduce-scatter.10
  289.6 38.2 reduce-scatter.8
  330.2 186.3 reduce-scatter.6
  518.8 186.2 reduce-scatter.4
where the time goes:
time: 728 us; the launch traced here: 726 us
  waiting for transfers between devices  625 us (86%)
  matrix products  50.2 us (7%)
  other arithmetic  23.6 us (3%)
  between operations  14.2 us (2%)
  local copies, waits for them, and re-layouts  12.4 us (2%)
    reduce_scatter x2, waiting for transfers between devices, per_device(): lax.psum_scatter(right_part.reshape(row_step, mesh_rows * BLOCK_SIZE, num...  369 us
    all_gather x2, waiting for transfers between devices, per_device(): lax.all_gather(side_block, 'row', axis=1)  195 us
    reduce_scatter x2, waiting for transfers between devices, per_device(): lax.psum_scatter(lower_part.reshape(left_rows, col_step, mesh_cols * BLOC...  50 us
    dot_general x2, matrix products, per_device(): jnp.einsum('rf,bqef->rbqe', grad_rows, side_rows, preferred_element_type=...  25.5 us
    dot_general x2, matrix products, per_device(): jnp.einsum('rbqe,rf->bqef', gathered, grad_rows, preferred_element_type=j...  24.7 us
  transfers between devices with their start and end apart: 8, of which 8 were waited for; matrix products, arithmetic and copies ran while one was open for 9% of the time, Pallas kernels for 0%

commit v1 on v0

v1 whole, which is shorter than its diff:
```python
import jax
import jax.numpy as jnp
from jax import lax
from jax.experimental import pallas as pl
from jax.experimental.pallas import tpu as pltpu
from jax.sharding import PartitionSpec as P

BLK = 256
F32 = jnp.float32
BF16 = jnp.bfloat16
MESH = pl.DeviceIdType.MESH
TILE = 512
EARLY = ((0, 2048),)
LATE = ((2048, 1024), (3072, 512), (3584, 512))
CHUNKS = EARLY + LATE
LOCAL_SLOTS = ((0, 0), (1, 0), (2, 0), (3, 0), (2, 1), (3, 1))
FAR_SLOTS = ((3, 0), (3, 1), (2, 0), (2, 1), (1, 0))
NUM_LOCAL = len(LOCAL_SLOTS)
NUM_SLOTS = NUM_LOCAL + len(FAR_SLOTS)
GROUPS = ((0, 6), (6, 8), (8, 10), (10, 11))


def rows(p, n=1):
    return pl.ds(p * BLK, n * BLK)


def kernel(lower, side, grad, db, dl, xr, xl, bl, acc, wl, wr, part, peer, cross, done, corner,
           bulk_s, bulk_r, load_s, wl_s, wl_r, near_s, near_r, far_s, far_r, push_s, push_r, cross_s, cross_r, back_s, back_r, corner_s, corner_r):
    r = lax.axis_index("row")
    c = lax.axis_index("col")
    x = c // 2
    core = c % 2
    own = core == r
    other = core != r
    across = {"row": 1 - r}
    mate = {"col": 2 * x + 1 - core}
    next_chip = {"col": 2 * (1 - x) + core}
    diagonal = {"col": 2 * (1 - x) + 1 - core}
    num_cols = grad.shape[1]
    sent = []

    def copy_to(device, src, dst, send_sem, recv_sem):
        return pltpu.make_async_remote_copy(src_ref=src, dst_ref=dst, send_sem=send_sem, recv_sem=recv_sem, device_id=device, device_id_type=MESH)

    def start(when, copy):
        sent.append((when, copy))
        if when is None:
            copy.start()
        else:
            pl.when(when)(copy.start)

    def arrived(ref, sem):
        pltpu.make_async_copy(ref, ref, sem).wait()

    barrier = pltpu.get_barrier_semaphore()
    for device in (across, mate, next_chip, diagonal):
        pl.semaphore_signal(barrier, inc=1, device_id=device, device_id_type=MESH)
    pl.semaphore_wait(barrier, 4)

    near_src = (lower.at[pl.ds(BLK, 3 * BLK), pl.ds(0, BLK)], lower.at[pl.ds(3 * BLK, BLK), pl.ds(BLK, BLK)])
    far_src = (lower.at[pl.ds(0, BLK), pl.ds(0, BLK)], lower.at[pl.ds(2 * BLK, BLK), pl.ds(BLK, BLK)])

    def near_dst(q, h):
        return wr.at[q, rows(1, 3)] if h == 0 else wr.at[q, rows(3)]

    def far_dst(q):
        return wr.at[q, rows(q)]

    for h in range(2):
        start(other, copy_to(across, near_src[h], near_dst(x + 2 * h, h), near_s.at[h], near_r.at[x + 2 * h]))
    far_sender = other & (r == 1) & (x == 0)
    for h in range(2):
        start(far_sender, copy_to(across, far_src[h], far_dst(2 * h), far_s.at[h], far_r.at[h]))

    def bulk(i, p):
        return copy_to(across, grad.at[rows(p)], xr.at[rows(p)], bulk_s.at[i], bulk_r.at[i])

    start(None, bulk(0, 3))
    start(None, bulk(1, 2))

    loads = [pltpu.make_async_copy(side.at[rows(q)], bl.at[rows(q)], load_s.at[q]) for q in range(4)]
    loads += [pltpu.make_async_copy(grad.at[rows(p)], xl.at[rows(p)], load_s.at[4 + p]) for p in range(4)]
    for load in loads:
        load.start()

    for h in range(2):
        src = lower.at[:, pl.ds(0, BLK)] if h == 0 else lower.at[rows(2, 2), pl.ds(BLK, BLK)]
        q = x + 2 * h
        dst = wl.at[q] if h == 0 else wl.at[q, rows(2, 2)]
        pl.when(own)(pltpu.make_async_copy(src, dst, wl_r.at[q]).start)
        for n, device in enumerate((mate, next_chip, diagonal)):
            start(own, copy_to(device, src, dst, wl_s.at[3 * h + n], wl_r.at[q]))

    @pl.when(r == 1)
    def _():
        wr[2, rows(2)] = jnp.zeros((BLK, BLK), BF16)

    for p in range(4):
        for h in range(2):
            far_zero = (x + 2 * h > p + r - 1) if p else (x >= 0)
            zero = (other & far_zero) | (own & (x + 2 * h > p))

            @pl.when(zero)
            def _():
                dl[rows(p), rows(h)] = jnp.zeros((BLK, BLK), BF16)

    def outer(left, left_row, q):
        total = None
        for k in range(0, num_cols, 1024):
            term = lax.dot_general(left[pl.ds(left_row, BLK), pl.ds(k, 1024)], bl[pl.ds(q * BLK, BLK), pl.ds(k, 1024)], (((1,), (1,)), ((), ())), preferred_element_type=F32)
            total = term if total is None else total + term
        return total

    for load in loads:
        load.wait()

    def local_outer(i, carry):
        slot, parity = i // 2, i % 2
        h = slot // 4
        p = slot - 2 * h
        part[slot, parity] = outer(xl, pl.multiple_of(p * BLK, BLK), 2 * h + parity)
        return carry

    lax.fori_loop(0, 2 * NUM_LOCAL, local_outer, 0)

    for h in range(2):
        q = x + 2 * h

        @pl.when(own)
        def _():
            arrived(near_dst(q, h), near_r.at[q])

        for n, device in enumerate((mate, next_chip, diagonal)):
            start(own, copy_to(device, near_dst(q, h), near_dst(q, h), near_s.at[2 + 3 * h + n], near_r.at[q]))
    far_owner = own & (r == 0) & (x == 0)
    for h in range(2):

        @pl.when(far_owner)
        def _():
            arrived(far_dst(2 * h), far_r.at[h])

        for n, device in enumerate((mate, next_chip, diagonal)):
            start(far_owner, copy_to(device, far_dst(2 * h), far_dst(2 * h), far_s.at[2 + 3 * h + n], far_r.at[h]))

    def push(g):
        lo, hi = GROUPS[g]
        span = pl.ds(lo, hi - lo)
        start(other, copy_to(mate, part.at[span], peer.at[span], push_s.at[g], push_r.at[g]))

    def add_and_cross(g):
        lo, hi = GROUPS[g]
        span = pl.ds(lo, hi - lo)

        @pl.when(own)
        def _():
            arrived(peer.at[span], push_r.at[g])

            def add(slot, carry):
                part[slot] = part[slot] + peer[slot]
                return carry

            lax.fori_loop(lo, hi, add, 0)

        start(own, copy_to(next_chip, part.at[span, 1 - x], cross.at[span], cross_s.at[g], cross_r.at[g]))

    def wait_cross(g):
        lo, hi = GROUPS[g]
        arrived(cross.at[pl.ds(lo, hi - lo)], cross_r.at[g])

    def back_copies(i):
        p, h = FAR_SLOTS[i]
        return copy_to(across, done.at[i], dl.at[rows(p), rows(h)], back_s.at[i], back_r.at[i])

    def finish_far(g):
        lo, hi = GROUPS[g]

        @pl.when(own)
        def _():
            wait_cross(g)
            for slot in range(lo, hi):
                done[slot - NUM_LOCAL] = (part[slot, x] + cross[slot]).astype(BF16)

        for slot in range(lo, hi):
            p, h = FAR_SLOTS[slot - NUM_LOCAL]
            start(own & (x + 2 * h <= p - r), back_copies(slot - NUM_LOCAL))

    def finish_local():
        @pl.when(own)
        def _():
            wait_cross(0)
            below = lax.broadcasted_iota(jnp.int32, (BLK, BLK), 0) >= lax.broadcasted_iota(jnp.int32, (BLK, BLK), 1)
            for slot, (p, h) in enumerate(LOCAL_SLOTS):
                q = x + 2 * h

                @pl.when(q <= p)
                def _():
                    total = part[slot, x] + cross[slot]
                    keep = below | (q < p)
                    dl[rows(p), rows(h)] = jnp.where(keep, total, 0.0).astype(BF16)

    def far_outer(p, lo, num_q):
        def body(q, carry):
            part[lo + q // 2, q % 2] = outer(xr, p * BLK, q)
            return carry

        lax.fori_loop(0, num_q, body, 0)

    def row_sum(q, far_first, cols):
        near = lax.dot_general(wl[q, rows(q, 4 - q)], xl[rows(q, 4 - q), cols], (((0,), (0,)), ((), ())), preferred_element_type=F32)
        far = lax.dot_general(wr[q, rows(far_first, 4 - far_first)], xr[rows(far_first, 4 - far_first), cols], (((0,), (0,)), ((), ())), preferred_element_type=F32)
        return near + far

    def tile_loop(body):
        def step(j, carry):
            body(pl.ds(pl.multiple_of(j * TILE, TILE), TILE))
            return carry

        lax.fori_loop(0, num_cols // TILE, step, 0)

    def weights_here(q):
        h = q // 2
        arrived(wl.at[q] if h == 0 else wl.at[q, rows(2, 2)], wl_r.at[q])
        if h == 0:
            pl.when(other | (x != q))(lambda: arrived(near_dst(q, h), near_r.at[q]))
        else:
            pl.when(other | (x + 2 != q))(lambda: arrived(near_dst(q, h), near_r.at[q]))
        if q % 2 == 0:
            pl.when((r == 0) & jnp.logical_not(far_owner))(lambda: arrived(far_dst(q), far_r.at[h]))

    def block_row(q):
        weights_here(q)

        def body(cols):
            db[rows(q), cols] = row_sum(q, q, cols).astype(BF16)

        tile_loop(body)

    def chunk_copy(i):
        first, width = CHUNKS[i]
        cols = pl.ds(first, width)
        sems = bulk_s.at[3 + i], bulk_r.at[3 + i]
        dst = xr.at[rows(0), cols]
        return copy_to(across, grad.at[rows(0), cols], dst, *sems), copy_to(across, side.at[rows(0), cols], dst, *sems)

    def start_chunks(when, span):
        for i in span:
            from_grad, from_side = chunk_copy(i)
            start(when & (r == 1), from_grad)
            start(when & (r == 0), from_side)

    arrived(xr.at[rows(3)], bulk_r.at[0])
    push(0)
    far_outer(3, 6, 4)
    block_row(3)
    start(None, bulk(2, 1))
    push(1)
    add_and_cross(0)
    add_and_cross(1)

    arrived(xr.at[rows(2)], bulk_r.at[1])
    finish_far(1)
    early = range(len(EARLY))
    late = range(len(EARLY), len(CHUNKS))
    start_chunks(core >= 0, early)
    far_outer(2, 8, 4)
    block_row(2)
    push(2)
    finish_local()
    add_and_cross(2)

    arrived(xr.at[rows(1)], bulk_r.at[2])
    last_sender = own & (r == 1)
    start_chunks(jnp.logical_not(last_sender), late)
    finish_far(2)
    far_outer(1, 10, 2)
    block_row(1)
    push(3)
    weights_here(0)

    def first_row(cols):
        total = row_sum(0, 1, cols)

        @pl.when(r == 1)
        def _():
            db[rows(0), cols] = total.astype(BF16)

        @pl.when(r == 0)
        def _():
            acc[:, cols] = total

    def first_half(lo, hi):
        def step(j, carry):
            first_row(pl.ds(pl.multiple_of(j * TILE, TILE), TILE))
            return carry

        lax.fori_loop(lo, hi, step, 0)

    add_and_cross(3)
    first_half(0, num_cols // TILE)
    finish_far(3)
    start_chunks(last_sender, late)

    @pl.when(r == 1)
    def _():
        corner[0] = jnp.zeros((BLK, BLK), F32)

    for i, (first, width) in enumerate(CHUNKS):
        arrived(xr.at[rows(0), pl.ds(first, width)], bulk_r.at[3 + i])

        def step(j, carry):
            cols = pl.ds(pl.multiple_of(first + j * TILE, TILE), TILE)

            @pl.when(r == 0)
            def _():
                term = lax.dot_general(wr[0, rows(0)], xr[rows(0), cols], (((0,), (0,)), ((), ())), preferred_element_type=F32)
                db[rows(0), cols] = (acc[:, cols] + term).astype(BF16)

            @pl.when(r == 1)
            def _():
                corner[0] += lax.dot_general(xl[rows(0), cols], xr[rows(0), cols], (((1,), (1,)), ((), ())), preferred_element_type=F32)

            return carry

        lax.fori_loop(0, width // TILE, step, 0)

    corner_owner = (r == 1) & (core == 0)
    start((r == 1) & (core == 1), copy_to(mate, corner.at[0], corner.at[1], corner_s.at[0], corner_r.at[0]))

    @pl.when(corner_owner)
    def _():
        arrived(corner.at[1], corner_r.at[0])
        corner[0] += corner[1]

    start(corner_owner & (x == 1), copy_to(next_chip, corner.at[0], corner.at[2], corner_s.at[1], corner_r.at[1]))

    @pl.when(corner_owner & (x == 0))
    def _():
        arrived(corner.at[2], corner_r.at[1])
        dl[rows(0), rows(0)] = (corner[0] + corner[2]).astype(BF16)

    for i, (p, h) in enumerate(FAR_SLOTS):
        pl.when(other & (x + 2 * h <= p + r - 1))(lambda: arrived(dl.at[rows(p), rows(h)], back_r.at[i]))
    for when, copy in sent:
        if when is None:
            copy.wait_send()
        else:
            pl.when(when)(copy.wait_send)


def per_device(lower, side, grad):
    num_rows, num_cols = grad.shape
    dma = pltpu.SemaphoreType.DMA
    num_bulk = 3 + len(CHUNKS)
    return pl.pallas_call(
        kernel,
        in_specs=[pl.BlockSpec(memory_space=pl.ANY)] * 3,
        out_specs=[pl.BlockSpec(memory_space=pltpu.VMEM)] * 2,
        out_shape=[pltpu.VMEM(grad.shape, BF16), pltpu.VMEM(lower.shape, BF16)],
        scratch_shapes=[
            pltpu.VMEM((num_rows, num_cols), BF16),
            pltpu.VMEM((num_rows, num_cols), BF16),
            pltpu.VMEM((num_rows, num_cols), BF16),
            pltpu.VMEM((BLK, num_cols), F32),
            pltpu.VMEM((4, 4 * BLK, BLK), BF16),
            pltpu.VMEM((4, 4 * BLK, BLK), BF16),
            pltpu.VMEM((NUM_SLOTS, 2, BLK, BLK), F32),
            pltpu.VMEM((NUM_SLOTS, 2, BLK, BLK), F32),
            pltpu.VMEM((NUM_SLOTS, BLK, BLK), F32),
            pltpu.VMEM((len(FAR_SLOTS), BLK, BLK), BF16),
            pltpu.VMEM((3, BLK, BLK), F32),
            dma((num_bulk,)), dma((num_bulk,)), dma((8,)), dma((6,)), dma((4,)), dma((8,)), dma((4,)), dma((8,)), dma((2,)),
            dma((4,)), dma((4,)), dma((4,)), dma((4,)), dma((5,)), dma((5,)), dma((2,)), dma((2,)),
        ],
        compiler_params=pltpu.CompilerParams(collective_id=0, has_side_effects=True, vmem_limit_bytes=54 * 1024 * 1024),
    )(lower, side, grad)


def solution(mesh):
    spec = P(("batch", "row"), "col")
    return jax.shard_map(per_device, mesh=mesh, in_specs=(spec, spec, spec), out_specs=(spec, spec), check_vma=False)
```

time: 728 us -> 206 us (0.28)
  the two profiles are of different devices: /device:TPU:1 before, /device:TPU:0 now
where the time goes in v1:
time: 206 us
  Pallas kernels  201 us (98%)
  local copies, waits for them, and re-layouts  4.37 us (2%)
    pallas_call x1, Pallas kernels, per_device(): pl.pallas_call(kernel, in_specs=[pl.BlockSpec(memory_space=pl.ANY)] * 3,...  201 us
    unnamed x2, local copies, waits for them, and re-layouts  4.37 us

profile of v1, /device:TPU:0, one launch (start us, length us, event | category | flops | bytes accessed | tf_op | source)
XLA Modules:
  0.0 205.8 jit_solution(4230048486382409942)
XLA Ops:
  0.6 200.8 %shard_map.50 = (bf16[1024,4096]{1,0:T(8,128)(2,1)S(1)}, bf16[1024,512]{1,0:T(8,128)(2,1)S(1)}) custom-call(bf16[1024,512]{1,0:T(8,128)(2,1)} %lower.1, bf16[1024,4096]{1,0:T(8,128)(2,1)} %side.1, bf16[1024,4096]{1,0:T(8,128)(2,1)} %grad.1), custom_call_target="tpu_custom_call" | custom-call | tf_op jit(solution)/shard_map/pallas_call | solution.py:354
  201.4 3.4 %copy.7 = bf16[1024,4096]{1,0:T(8,128)(2,1)} copy(bf16[1024,4096]{1,0:T(8,128)(2,1)S(1)} %get-tuple-element.2) | data formatting | bytes 16777216
  204.8 1.0 copy.8

commit v2 on v1

--- a/solution.py
+++ b/solution.py
@@ -24,8 +24,8 @@
     return pl.ds(p * BLK, n * BLK)
 
 
-def kernel(lower, side, grad, db, dl, xr, xl, bl, acc, wl, wr, part, peer, cross, done, corner,
-           bulk_s, bulk_r, load_s, wl_s, wl_r, near_s, near_r, far_s, far_r, push_s, push_r, cross_s, cross_r, back_s, back_r, corner_s, corner_r):
+def kernel(lower, side, grad, db, dl, xr, xl, bl, acc, wl, wr, relay, part, peer, cross, done, corner,
+           bulk_s, bulk_r, load_s, wl_s, wl_r, near_s, near_r, far_s, far_r, relay_s, relay_r, push_s, push_r, cross_s, cross_r, back_s, back_r, corner_s, corner_r):
     r = lax.axis_index("row")
     c = lax.axis_index("col")
     x = c // 2
@@ -70,13 +70,12 @@
         start(other, copy_to(across, near_src[h], near_dst(x + 2 * h, h), near_s.at[h], near_r.at[x + 2 * h]))
     far_sender = other & (r == 1) & (x == 0)
     for h in range(2):
-        start(far_sender, copy_to(across, far_src[h], far_dst(2 * h), far_s.at[h], far_r.at[h]))
+        start(far_sender, copy_to(next_chip, far_src[h], relay.at[h], far_s.at[h], relay_r.at[h]))
 
     def bulk(i, p):
         return copy_to(across, grad.at[rows(p)], xr.at[rows(p)], bulk_s.at[i], bulk_r.at[i])
 
     start(None, bulk(0, 3))
-    start(None, bulk(1, 2))
 
     loads = [pltpu.make_async_copy(side.at[rows(q)], bl.at[rows(q)], load_s.at[q]) for q in range(4)]
     loads += [pltpu.make_async_copy(grad.at[rows(p)], xl.at[rows(p)], load_s.at[4 + p]) for p in range(4)]
@@ -132,15 +131,16 @@
 
         for n, device in enumerate((mate, next_chip, diagonal)):
             start(own, copy_to(device, near_dst(q, h), near_dst(q, h), near_s.at[2 + 3 * h + n], near_r.at[q]))
-    far_owner = own & (r == 0) & (x == 0)
-    for h in range(2):
-
-        @pl.when(far_owner)
-        def _():
-            arrived(far_dst(2 * h), far_r.at[h])
-
-        for n, device in enumerate((mate, next_chip, diagonal)):
-            start(far_owner, copy_to(device, far_dst(2 * h), far_dst(2 * h), far_s.at[2 + 3 * h + n], far_r.at[h]))
+    far_owner = own & (r == 0) & (x == 1)
+    relay_here = other & (r == 1) & (x == 1)
+    for h in range(2):
+
+        @pl.when(relay_here)
+        def _():
+            arrived(relay.at[h], relay_r.at[h])
+
+        start(relay_here, copy_to(across, relay.at[h], far_dst(2 * h), relay_s.at[h], far_r.at[h]))
+    start(None, bulk(1, 2))
 
     def push(g):
         lo, hi = GROUPS[g]
@@ -235,24 +235,31 @@
 
         tile_loop(body)
 
-    def chunk_copy(i):
+    def chunk_copy(i, source):
         first, width = CHUNKS[i]
         cols = pl.ds(first, width)
         sems = bulk_s.at[3 + i], bulk_r.at[3 + i]
-        dst = xr.at[rows(0), cols]
-        return copy_to(across, grad.at[rows(0), cols], dst, *sems), copy_to(across, side.at[rows(0), cols], dst, *sems)
+        return copy_to(across, source.at[rows(0), cols], xr.at[rows(0), cols], *sems)
 
     def start_chunks(when, span):
         for i in span:
-            from_grad, from_side = chunk_copy(i)
-            start(when & (r == 1), from_grad)
-            start(when & (r == 0), from_side)
+            start(when & (r == 1), chunk_copy(i, grad))
+            if CHUNKS[i] in LATE:
+                start(when & (r == 0), chunk_copy(i, side))
 
     arrived(xr.at[rows(3)], bulk_r.at[0])
     push(0)
     far_outer(3, 6, 4)
     block_row(3)
     start(None, bulk(2, 1))
+    for h in range(2):
+
+        @pl.when(far_owner)
+        def _():
+            arrived(far_dst(2 * h), far_r.at[h])
+
+        for n, device in enumerate((mate, next_chip, diagonal)):
+            start(far_owner, copy_to(device, far_dst(2 * h), far_dst(2 * h), far_s.at[2 + 3 * h + n], far_r.at[h]))
     push(1)
     add_and_cross(0)
     add_and_cross(1)
@@ -300,43 +307,71 @@
     finish_far(3)
     start_chunks(last_sender, late)
 
-    @pl.when(r == 1)
+    corner[0] = jnp.zeros((BLK, BLK), F32)
+
+    def nt_dot(left, right):
+        return lax.dot_general(left, right, (((1,), (1,)), ((), ())), preferred_element_type=F32)
+
+    def corner_in_row(row):
+        start((r == row) & (core == 1), copy_to(mate, corner.at[0], corner.at[1], corner_s.at[0], corner_r.at[0]))
+        owner = (r == row) & (core == 0)
+
+        @pl.when(owner)
+        def _():
+            arrived(corner.at[1], corner_r.at[0])
+            corner[0] += corner[1]
+
+        start(owner & (x == 1), copy_to(next_chip, corner.at[0], corner.at[2], corner_s.at[1], corner_r.at[1]))
+
+        @pl.when(owner & (x == 0))
+        def _():
+            arrived(corner.at[2], corner_r.at[1])
+
+        return owner & (x == 0)
+
+    for i, (first, width) in enumerate(CHUNKS):
+        early_chunk = (first, width) in EARLY
+        here = (r == 0) if early_chunk else (r >= 0)
+
+        @pl.when(here)
+        def _():
+            arrived(xr.at[rows(0), pl.ds(first, width)], bulk_r.at[3 + i])
+
+            def step(j, carry):
+                cols = pl.ds(pl.multiple_of(first + j * TILE, TILE), TILE)
+
+                @pl.when(r == 0)
+                def _():
+                    term = lax.dot_general(wr[0, rows(0)], xr[rows(0), cols], (((0,), (0,)), ((), ())), preferred_element_type=F32)
+                    db[rows(0), cols] = (acc[:, cols] + term).astype(BF16)
+                    if early_chunk:
+                        corner[0] += nt_dot(xr[rows(0), cols], bl[rows(0), cols])
+
+                if not early_chunk:
+
+                    @pl.when(r == 1)
+                    def _():
+                        corner[0] += nt_dot(xl[rows(0), cols], xr[rows(0), cols])
+
+                return carry
+
+            lax.fori_loop(0, width // TILE, step, 0)
+
+        if i == len(EARLY) - 1:
+            first_device = corner_in_row(0)
+
+            @pl.when(first_device)
+            def _():
+                corner[0] += corner[2]
+
+            start(first_device, copy_to(across, corner.at[0], corner.at[3], corner_s.at[2], corner_r.at[2]))
+
+    last_device = corner_in_row(1)
+
+    @pl.when(last_device)
     def _():
-        corner[0] = jnp.zeros((BLK, BLK), F32)
-
-    for i, (first, width) in enumerate(CHUNKS):
-        arrived(xr.at[rows(0), pl.ds(first, width)], bulk_r.at[3 + i])
-
-        def step(j, carry):
-            cols = pl.ds(pl.multiple_of(first + j * TILE, TILE), TILE)
-
-            @pl.when(r == 0)
-            def _():
-                term = lax.dot_general(wr[0, rows(0)], xr[rows(0), cols], (((0,), (0,)), ((), ())), preferred_element_type=F32)
-                db[rows(0), cols] = (acc[:, cols] + term).astype(BF16)
-
-            @pl.when(r == 1)
-            def _():
-                corner[0] += lax.dot_general(xl[rows(0), cols], xr[rows(0), cols], (((1,), (1,)), ((), ())), preferred_element_type=F32)
-
-            return carry
-
-        lax.fori_loop(0, width // TILE, step, 0)
-
-    corner_owner = (r == 1) & (core == 0)
-    start((r == 1) & (core == 1), copy_to(mate, corner.at[0], corner.at[1], corner_s.at[0], corner_r.at[0]))
-
-    @pl.when(corner_owner)
-    def _():
-        arrived(corner.at[1], corner_r.at[0])
-        corner[0] += corner[1]
-
-    start(corner_owner & (x == 1), copy_to(next_chip, corner.at[0], corner.at[2], corner_s.at[1], corner_r.at[1]))
-
-    @pl.when(corner_owner & (x == 0))
-    def _():
-        arrived(corner.at[2], corner_r.at[1])
-        dl[rows(0), rows(0)] = (corner[0] + corner[2]).astype(BF16)
+        arrived(corner.at[3], corner_r.at[2])
+        dl[rows(0), rows(0)] = (corner[0] + corner[2] + corner[3]).astype(BF16)
 
     for i, (p, h) in enumerate(FAR_SLOTS):
         pl.when(other & (x + 2 * h <= p + r - 1))(lambda: arrived(dl.at[rows(p), rows(h)], back_r.at[i]))
@@ -363,13 +398,14 @@
             pltpu.VMEM((BLK, num_cols), F32),
             pltpu.VMEM((4, 4 * BLK, BLK), BF16),
             pltpu.VMEM((4, 4 * BLK, BLK), BF16),
+            pltpu.VMEM((2, BLK, BLK), BF16),
             pltpu.VMEM((NUM_SLOTS, 2, BLK, BLK), F32),
             pltpu.VMEM((NUM_SLOTS, 2, BLK, BLK), F32),
             pltpu.VMEM((NUM_SLOTS, BLK, BLK), F32),
             pltpu.VMEM((len(FAR_SLOTS), BLK, BLK), BF16),
-            pltpu.VMEM((3, BLK, BLK), F32),
-            dma((num_bulk,)), dma((num_bulk,)), dma((8,)), dma((6,)), dma((4,)), dma((8,)), dma((4,)), dma((8,)), dma((2,)),
-            dma((4,)), dma((4,)), dma((4,)), dma((4,)), dma((5,)), dma((5,)), dma((2,)), dma((2,)),
+            pltpu.VMEM((4, BLK, BLK), F32),
+            dma((num_bulk,)), dma((num_bulk,)), dma((8,)), dma((6,)), dma((4,)), dma((8,)), dma((4,)), dma((8,)), dma((2,)), dma((2,)), dma((2,)),
+            dma((4,)), dma((4,)), dma((4,)), dma((4,)), dma((5,)), dma((5,)), dma((3,)), dma((3,)),
         ],
         compiler_params=pltpu.CompilerParams(collective_id=0, has_side_effects=True, vmem_limit_bytes=54 * 1024 * 1024),
     )(lower, side, grad)

time: 206 us -> 203 us (0.985)
  the two profiles are of different devices: /device:TPU:0 before, /device:TPU:1 now
where the time goes in v2:
time: 203 us; the launch traced here: 202 us
  Pallas kernels  197 us (97%)
  local copies, waits for them, and re-layouts  4.37 us (2%)
    pallas_call x1, Pallas kernels, per_device(): pl.pallas_call(kernel, in_specs=[pl.BlockSpec(memory_space=pl.ANY)] * 3,...  197 us
    unnamed x2, local copies, waits for them, and re-layouts  4.37 us

profile of v2, /device:TPU:1, one launch (start us, length us, event | category | flops | bytes accessed | tf_op | source)
XLA Modules:
  0.0 201.7 jit_solution(933400949852826536)
XLA Ops:
  0.6 196.7 %shard_map.50 = (bf16[1024,4096]{1,0:T(8,128)(2,1)S(1)}, bf16[1024,512]{1,0:T(8,128)(2,1)S(1)}) custom-call(bf16[1024,512]{1,0:T(8,128)(2,1)} %lower.1, bf16[1024,4096]{1,0:T(8,128)(2,1)} %side.1, bf16[1024,4096]{1,0:T(8,128)(2,1)} %grad.1), custom_call_target="tpu_custom_call" | custom-call | tf_op jit(solution)/shard_map/pallas_call | solution.py:389
  197.3 3.4 %copy.7 = bf16[1024,4096]{1,0:T(8,128)(2,1)} copy(bf16[1024,4096]{1,0:T(8,128)(2,1)S(1)} %get-tuple-element.2) | data formatting | bytes 16777216
  200.7 1.0 copy.8

commit v3 on v2

--- a/solution.py
+++ b/solution.py
@@ -53,9 +53,18 @@
         pltpu.make_async_copy(ref, ref, sem).wait()
 
     barrier = pltpu.get_barrier_semaphore()
-    for device in (across, mate, next_chip, diagonal):
-        pl.semaphore_signal(barrier, inc=1, device_id=device, device_id_type=MESH)
-    pl.semaphore_wait(barrier, 4)
+
+    def greet(when, *devices):
+        @pl.when(when)
+        def _():
+            for device in devices:
+                pl.semaphore_signal(barrier, inc=1, device_id=device, device_id_type=MESH)
+
+    first_core = core == 0
+    second_core = core == 1
+    greet(first_core, across)
+    greet(second_core, across, next_chip)
+    pl.when(first_core)(lambda: pl.semaphore_wait(barrier, 1))
 
     near_src = (lower.at[pl.ds(BLK, 3 * BLK), pl.ds(0, BLK)], lower.at[pl.ds(3 * BLK, BLK), pl.ds(BLK, BLK)])
     far_src = (lower.at[pl.ds(0, BLK), pl.ds(0, BLK)], lower.at[pl.ds(2 * BLK, BLK), pl.ds(BLK, BLK)])
@@ -66,16 +75,24 @@
     def far_dst(q):
         return wr.at[q, rows(q)]
 
-    for h in range(2):
-        start(other, copy_to(across, near_src[h], near_dst(x + 2 * h, h), near_s.at[h], near_r.at[x + 2 * h]))
+    def bulk(i, p):
+        return copy_to(across, grad.at[rows(p)], xr.at[rows(p)], bulk_s.at[i], bulk_r.at[i])
+
+    def first_copies(when):
+        for h in range(2):
+            start(when & other, copy_to(across, near_src[h], near_dst(x + 2 * h, h), near_s.at[h], near_r.at[x + 2 * h]))
+        start(when, bulk(0, 3))
+
+    first_copies(first_core)
+    greet(first_core, mate, diagonal)
+    pl.when(second_core)(lambda: pl.semaphore_wait(barrier, 4))
+    first_copies(second_core)
+    greet(second_core, mate)
+    pl.when(first_core)(lambda: pl.semaphore_wait(barrier, 1))
+
     far_sender = other & (r == 1) & (x == 0)
     for h in range(2):
         start(far_sender, copy_to(next_chip, far_src[h], relay.at[h], far_s.at[h], relay_r.at[h]))
-
-    def bulk(i, p):
-        return copy_to(across, grad.at[rows(p)], xr.at[rows(p)], bulk_s.at[i], bulk_r.at[i])
-
-    start(None, bulk(0, 3))
 
     loads = [pltpu.make_async_copy(side.at[rows(q)], bl.at[rows(q)], load_s.at[q]) for q in range(4)]
     loads += [pltpu.make_async_copy(grad.at[rows(p)], xl.at[rows(p)], load_s.at[4 + p]) for p in range(4)]
@@ -386,7 +403,7 @@
     num_rows, num_cols = grad.shape
     dma = pltpu.SemaphoreType.DMA
     num_bulk = 3 + len(CHUNKS)
-    return pl.pallas_call(
+    results = pl.pallas_call(
         kernel,
         in_specs=[pl.BlockSpec(memory_space=pl.ANY)] * 3,
         out_specs=[pl.BlockSpec(memory_space=pltpu.VMEM)] * 2,
@@ -409,6 +426,24 @@
         ],
         compiler_params=pltpu.CompilerParams(collective_id=0, has_side_effects=True, vmem_limit_bytes=54 * 1024 * 1024),
     )(lower, side, grad)
+    pieces = 4
+    return pl.pallas_call(
+        put_kernel,
+        in_specs=[pl.BlockSpec(memory_space=pltpu.VMEM)] * 2,
+        out_specs=[pl.BlockSpec(memory_space=pl.ANY)] * 2,
+        out_shape=[jax.ShapeDtypeStruct(grad.shape, BF16), jax.ShapeDtypeStruct(lower.shape, BF16)],
+        scratch_shapes=[dma((pieces + 1,))],
+        compiler_params=pltpu.CompilerParams(vmem_limit_bytes=1024 * 1024),
+    )(*[pltpu.with_memory_space_constraint(v, pltpu.VMEM) for v in results])
+
+
+def put_kernel(db_in, dl_in, db_out, dl_out, sems):
+    copies = [pltpu.make_async_copy(dl_in, dl_out, sems.at[0])]
+    copies += [pltpu.make_async_copy(db_in.at[rows(i)], db_out.at[rows(i)], sems.at[1 + i]) for i in range(4)]
+    for copy in copies:
+        copy.start()
+    for copy in copies:
+        copy.wait()
 
 
 def solution(mesh):

time: 203 us -> 201 us (level)
  local copies, waits for them, and re-layouts: 4.37 us -> 0 us
  Pallas kernels: 197 us -> 200 us
    unnamed x2 -> x0, local copies, waits for them, and re-layouts: 4.37 us -> none
    pallas_call x0 -> x1, Pallas kernels: none -> 3.72 us  [per_device(): pl.pallas_call(put_kernel, in_specs=[pl.BlockSpec(memory_space=pltpu.VMEM...]
where the time goes in v3:
time: 201 us; the launch traced here: 200 us
  Pallas kernels  200 us (100%)
    pallas_call x1, Pallas kernels, per_device(): pl.pallas_call(kernel, in_specs=[pl.BlockSpec(memory_space=pl.ANY)] * 3,...  196 us

profile of v3, /device:TPU:1, one launch (start us, length us, event | category | flops | bytes accessed | tf_op | source)
XLA Modules:
  0.0 200.4 jit_solution(15899098756344749503)
XLA Ops:
  0.6 196.1 %shard_map.50 = (bf16[1024,4096]{1,0:T(8,128)(2,1)S(1)}, bf16[1024,512]{1,0:T(8,128)(2,1)S(1)}) custom-call(bf16[1024,512]{1,0:T(8,128)(2,1)} %lower.1, bf16[1024,4096]{1,0:T(8,128)(2,1)} %side.1, bf16[1024,4096]{1,0:T(8,128)(2,1)} %grad.1), custom_call_target="tpu_custom_call" | custom-call | tf_op jit(solution)/shard_map/pallas_call | solution.py:406
  196.7 3.7 %shard_map.51 = (bf16[1024,4096]{1,0:T(8,128)(2,1)}, bf16[1024,512]{1,0:T(8,128)(2,1)}) custom-call(bf16[1024,4096]{1,0:T(8,128)(2,1)S(1)} %get-tuple-element.4.db_in, bf16[1024,512]{1,0:T(8,128)(2,1)S(1)} %get-tuple-element.5.dl_in), custom_call_target="tpu_custom_call" | custom-call | tf_op jit(solution)/shard_map/pallas_call | solution.py:430

commit v4 on v3

--- a/solution.py
+++ b/solution.py
@@ -24,7 +24,7 @@
     return pl.ds(p * BLK, n * BLK)
 
 
-def kernel(lower, side, grad, db, dl, xr, xl, bl, acc, wl, wr, relay, part, peer, cross, done, corner,
+def kernel(lower, side, grad, db, dl, acc, corner_weight, xr, xl, bl, wl, wr, relay, part, peer, cross, done, corner,
            bulk_s, bulk_r, load_s, wl_s, wl_r, near_s, near_r, far_s, far_r, relay_s, relay_r, push_s, push_r, cross_s, cross_r, back_s, back_r, corner_s, corner_r):
     r = lax.axis_index("row")
     c = lax.axis_index("col")
@@ -92,7 +92,7 @@
 
     far_sender = other & (r == 1) & (x == 0)
     for h in range(2):
-        start(far_sender, copy_to(next_chip, far_src[h], relay.at[h], far_s.at[h], relay_r.at[h]))
+        start(far_sender, copy_to(diagonal, far_src[h], relay.at[h], far_s.at[h], relay_r.at[h]))
 
     loads = [pltpu.make_async_copy(side.at[rows(q)], bl.at[rows(q)], load_s.at[q]) for q in range(4)]
     loads += [pltpu.make_async_copy(grad.at[rows(p)], xl.at[rows(p)], load_s.at[4 + p]) for p in range(4)]
@@ -148,8 +148,8 @@
 
         for n, device in enumerate((mate, next_chip, diagonal)):
             start(own, copy_to(device, near_dst(q, h), near_dst(q, h), near_s.at[2 + 3 * h + n], near_r.at[q]))
-    far_owner = own & (r == 0) & (x == 1)
-    relay_here = other & (r == 1) & (x == 1)
+    far_owner = other & (r == 0) & (x == 1)
+    relay_here = own & (r == 1) & (x == 1)
     for h in range(2):
 
         @pl.when(relay_here)
@@ -258,11 +258,12 @@
         sems = bulk_s.at[3 + i], bulk_r.at[3 + i]
         return copy_to(across, source.at[rows(0), cols], xr.at[rows(0), cols], *sems)
 
-    def start_chunks(when, span):
+    def start_chunks(span):
         for i in span:
-            start(when & (r == 1), chunk_copy(i, grad))
-            if CHUNKS[i] in LATE:
-                start(when & (r == 0), chunk_copy(i, side))
+            late_chunk = CHUNKS[i] in LATE
+            start((r == 1) & (core == 0) if late_chunk else r == 1, chunk_copy(i, grad))
+            if late_chunk:
+                start(r == 0, chunk_copy(i, side))
 
     arrived(xr.at[rows(3)], bulk_r.at[0])
     push(0)
@@ -285,7 +286,7 @@
     finish_far(1)
     early = range(len(EARLY))
     late = range(len(EARLY), len(CHUNKS))
-    start_chunks(core >= 0, early)
+    start_chunks(early)
     far_outer(2, 8, 4)
     block_row(2)
     push(2)
@@ -293,14 +294,17 @@
     add_and_cross(2)
 
     arrived(xr.at[rows(1)], bulk_r.at[2])
-    last_sender = own & (r == 1)
-    start_chunks(jnp.logical_not(last_sender), late)
+    start_chunks(late)
     finish_far(2)
     far_outer(1, 10, 2)
     block_row(1)
     push(3)
     weights_here(0)
 
+    @pl.when(r == 0)
+    def _():
+        corner_weight[...] = wr[0, rows(0)]
+
     def first_row(cols):
         total = row_sum(0, 1, cols)
 
@@ -322,7 +326,6 @@
     add_and_cross(3)
     first_half(0, num_cols // TILE)
     finish_far(3)
-    start_chunks(last_sender, late)
 
     corner[0] = jnp.zeros((BLK, BLK), F32)
 
@@ -348,7 +351,7 @@
 
     for i, (first, width) in enumerate(CHUNKS):
         early_chunk = (first, width) in EARLY
-        here = (r == 0) if early_chunk else (r >= 0)
+        here = (r == 0) if early_chunk else (r == 1) | (core == 0)
 
         @pl.when(here)
         def _():
@@ -403,16 +406,15 @@
     num_rows, num_cols = grad.shape
     dma = pltpu.SemaphoreType.DMA
     num_bulk = 3 + len(CHUNKS)
-    results = pl.pallas_call(
+    db, dl, acc, weight = pl.pallas_call(
         kernel,
         in_specs=[pl.BlockSpec(memory_space=pl.ANY)] * 3,
-        out_specs=[pl.BlockSpec(memory_space=pltpu.VMEM)] * 2,
-        out_shape=[pltpu.VMEM(grad.shape, BF16), pltpu.VMEM(lower.shape, BF16)],
+        out_specs=[pl.BlockSpec(memory_space=pltpu.VMEM)] * 4,
+        out_shape=[pltpu.VMEM(grad.shape, BF16), pltpu.VMEM(lower.shape, BF16), pltpu.VMEM((BLK, num_cols), F32), pltpu.VMEM((BLK, BLK), BF16)],
         scratch_shapes=[
             pltpu.VMEM((num_rows, num_cols), BF16),
             pltpu.VMEM((num_rows, num_cols), BF16),
             pltpu.VMEM((num_rows, num_cols), BF16),
-            pltpu.VMEM((BLK, num_cols), F32),
             pltpu.VMEM((4, 4 * BLK, BLK), BF16),
             pltpu.VMEM((4, 4 * BLK, BLK), BF16),
             pltpu.VMEM((2, BLK, BLK), BF16),
@@ -424,17 +426,46 @@
             dma((num_bulk,)), dma((num_bulk,)), dma((8,)), dma((6,)), dma((4,)), dma((8,)), dma((4,)), dma((8,)), dma((2,)), dma((2,)), dma((2,)),
             dma((4,)), dma((4,)), dma((4,)), dma((4,)), dma((5,)), dma((5,)), dma((3,)), dma((3,)),
         ],
-        compiler_params=pltpu.CompilerParams(collective_id=0, has_side_effects=True, vmem_limit_bytes=54 * 1024 * 1024),
+        compiler_params=pltpu.CompilerParams(collective_id=0, has_side_effects=True, vmem_limit_bytes=49 * 1024 * 1024),
     )(lower, side, grad)
-    pieces = 4
-    return pl.pallas_call(
+    in_vmem = pl.BlockSpec(memory_space=pltpu.VMEM)
+    anywhere = pl.BlockSpec(memory_space=pl.ANY)
+
+    def keep(value):
+        return pltpu.with_memory_space_constraint(value, pltpu.VMEM)
+
+    in_hbm = pl.BlockSpec(memory_space=pltpu.HBM)
+
+    def stay(value):
+        return pltpu.with_memory_space_constraint(value, pltpu.HBM)
+
+    db, dl = pl.pallas_call(
         put_kernel,
-        in_specs=[pl.BlockSpec(memory_space=pltpu.VMEM)] * 2,
-        out_specs=[pl.BlockSpec(memory_space=pl.ANY)] * 2,
+        in_specs=[in_vmem] * 2,
+        out_specs=[anywhere] * 2,
         out_shape=[jax.ShapeDtypeStruct(grad.shape, BF16), jax.ShapeDtypeStruct(lower.shape, BF16)],
-        scratch_shapes=[dma((pieces + 1,))],
+        scratch_shapes=[dma((5,))],
         compiler_params=pltpu.CompilerParams(vmem_limit_bytes=1024 * 1024),
-    )(*[pltpu.with_memory_space_constraint(v, pltpu.VMEM) for v in results])
+    )(keep(db), keep(dl))
+    width = sum(w for _, w in LATE)
+    tail = pl.pallas_call(
+        tail_kernel,
+        in_specs=[in_hbm, in_vmem, in_vmem, in_hbm],
+        out_specs=in_vmem,
+        out_shape=pltpu.VMEM((BLK, width), BF16),
+        scratch_shapes=[pltpu.VMEM((BLK, width), BF16), dma((len(LATE),)), dma((len(LATE),))],
+        compiler_params=pltpu.CompilerParams(collective_id=1, has_side_effects=True, vmem_limit_bytes=4 * 1024 * 1024),
+    )(stay(grad), keep(acc), keep(weight), stay(dl))
+    db = pl.pallas_call(
+        put_tail_kernel,
+        in_specs=[anywhere, in_vmem],
+        out_specs=anywhere,
+        out_shape=jax.ShapeDtypeStruct(grad.shape, BF16),
+        input_output_aliases={0: 0},
+        scratch_shapes=[dma],
+        compiler_params=pltpu.CompilerParams(vmem_limit_bytes=1024 * 1024),
+    )(db, keep(tail))
+    return db, dl
 
 
 def put_kernel(db_in, dl_in, db_out, dl_out, sems):
@@ -446,6 +477,45 @@
         copy.wait()
 
 
+def tail_kernel(grad, acc, weight, dl, tail, arriving, send_sem, recv_sem):
+    del dl
+    r = lax.axis_index("row")
+    core = lax.axis_index("col") % 2
+    sender = (r == 1) & (core == 1)
+    receiver = (r == 0) & (core == 1)
+    barrier = pltpu.get_barrier_semaphore()
+    pl.when(receiver)(lambda: pl.semaphore_signal(barrier, inc=1, device_id={"row": 1 - r}, device_id_type=MESH))
+    pl.when(sender)(lambda: pl.semaphore_wait(barrier, 1))
+    base = LATE[0][0]
+    copies = []
+    for i, (first, width) in enumerate(LATE):
+        copies.append(pltpu.make_async_remote_copy(
+            src_ref=grad.at[rows(0), pl.ds(first, width)], dst_ref=arriving.at[:, pl.ds(first - base, width)],
+            send_sem=send_sem.at[i], recv_sem=recv_sem.at[i], device_id={"row": 1 - r}, device_id_type=MESH))
+        pl.when(sender)(copies[i].start)
+    for i, (first, width) in enumerate(LATE):
+
+        @pl.when(receiver)
+        def _():
+            copies[i].wait_recv()
+            for n in range(width // TILE):
+                at = first - base + n * TILE
+                term = lax.dot_general(weight[...], arriving[:, pl.ds(at, TILE)], (((0,), (0,)), ((), ())), preferred_element_type=F32)
+                tail[:, pl.ds(at, TILE)] = (acc[:, pl.ds(base + at, TILE)] + term).astype(BF16)
+
+        pl.when(sender)(copies[i].wait_send)
+
+
+def put_tail_kernel(db_in, tail, db_out, sem):
+    del db_in
+
+    @pl.when((lax.axis_index("row") == 0) & (lax.axis_index("col") % 2 == 1))
+    def _():
+        copy = pltpu.make_async_copy(tail, db_out.at[rows(0), pl.ds(LATE[0][0], tail.shape[1])], sem)
+        copy.start()
+        copy.wait()
+
+
 def solution(mesh):
     spec = P(("batch", "row"), "col")
     return jax.shard_map(per_device, mesh=mesh, in_specs=(spec, spec, spec), out_specs=(spec, spec), check_vma=False)

time: 201 us -> 197 us (0.980)
  Pallas kernels: 200 us -> 196 us
    pallas_call x1, Pallas kernels: 196 us -> 175 us  [per_device(): pl.pallas_call(kernel, in_specs=[pl.BlockSpec(memory_space=pl.ANY)] * 3,...]
    pallas_call x1 -> x3, Pallas kernels: 3.72 us -> 21.2 us  [the longest x1 16.5 us: per_device(): pl.pallas_call(tail_kernel, in_specs=[in_hbm, in_vmem, in_vmem, in_hbm],...]
where the time goes in v4:
time: 197 us
  Pallas kernels  196 us (99%)
    pallas_call x1, Pallas kernels, per_device(): pl.pallas_call(kernel, in_specs=[pl.BlockSpec(memory_space=pl.ANY)] * 3,...  175 us
    pallas_call x1, Pallas kernels, per_device(): pl.pallas_call(tail_kernel, in_specs=[in_hbm, in_vmem, in_vmem, in_hbm],...  16.5 us

profile of v4, /device:TPU:1, one launch (start us, length us, event | category | flops | bytes accessed | tf_op | source)
XLA Modules:
  0.0 196.9 jit_solution(4085755481952925421)
XLA Ops:
  0.6 175.0 %shard_map.50 = (bf16[1024,4096]{1,0:T(8,128)(2,1)S(1)}, bf16[1024,512]{1,0:T(8,128)(2,1)S(1)}, f32[256,4096]{1,0:T(8,128)S(1)}, bf16[256,256]{1,0:T(8,128)(2,1)S(1)}) custom-call(bf16[1024,512]{1,0:T(8,128)(2,1)} %lower.1, bf16[1024,4096]{1,0:T(8,128)(2,1)} %side.1, bf16[1024,4096]{1,0:T(8,128)(2,1)} %grad.3), custom_call_target="tpu_custom_call" | custom-call | tf_op jit(solution)/shard_map/pallas_call | solution.py:409
  175.6 3.7 %shard_map.51 = (bf16[1024,4096]{1,0:T(8,128)(2,1)}, bf16[1024,512]{1,0:T(8,128)(2,1)}) custom-call(bf16[1024,4096]{1,0:T(8,128)(2,1)S(1)} %get-tuple-element.8.db_in, bf16[1024,512]{1,0:T(8,128)(2,1)S(1)} %get-tuple-element.9.dl_in), custom_call_target="tpu_custom_call" | custom-call | tf_op jit(solution)/shard_map/pallas_call | solution.py:442
  179.3 16.5 %shard_map.52.tail = bf16[256,2048]{1,0:T(8,128)(2,1)S(1)} custom-call(bf16[1024,4096]{1,0:T(8,128)(2,1)} %grad.3, f32[256,4096]{1,0:T(8,128)S(1)} %get-tuple-element.11.acc, bf16[256,256]{1,0:T(8,128)(2,1)S(1)} %get-tuple-element.12.weight, bf16[1024,512]{1,0:T(8,128)(2,1)} %get-tuple-element.7.dl), custom_call_target="tpu_custom_call" | custom-call | tf_op jit(solution)/shard_map/pallas_call | solution.py:451
  195.9 1.0 shard_map.53

commit v5 on v4

--- a/solution.py
+++ b/solution.py
@@ -9,9 +9,9 @@
 F32 = jnp.float32
 BF16 = jnp.bfloat16
 MESH = pl.DeviceIdType.MESH
-TILE = 512
-EARLY = ((0, 2048),)
-LATE = ((2048, 1024), (3072, 512), (3584, 512))
+TILE = 256
+EARLY = ((0, 2304),)
+LATE = ((2304, 1536), (3840, 256),)
 CHUNKS = EARLY + LATE
 LOCAL_SLOTS = ((0, 0), (1, 0), (2, 0), (3, 0), (2, 1), (3, 1))
 FAR_SLOTS = ((3, 0), (3, 1), (2, 0), (2, 1), (1, 0))
@@ -60,8 +60,8 @@
             for device in devices:
                 pl.semaphore_signal(barrier, inc=1, device_id=device, device_id_type=MESH)
 
-    first_core = core == 0
-    second_core = core == 1
+    first_core = core == 1
+    second_core = core == 0
     greet(first_core, across)
     greet(second_core, across, next_chip)
     pl.when(first_core)(lambda: pl.semaphore_wait(barrier, 1))

time: 197 us -> 196 us (level)
  no operation moved by 1% of the time
where the time goes in v5:
time: 196 us
  Pallas kernels  195 us (99%)
    pallas_call x1, Pallas kernels, per_device(): pl.pallas_call(kernel, in_specs=[pl.BlockSpec(memory_space=pl.ANY)] * 3,...  173 us
    pallas_call x1, Pallas kernels, per_device(): pl.pallas_call(tail_kernel, in_specs=[in_hbm, in_vmem, in_vmem, in_hbm],...  17.4 us

profile of v5, /device:TPU:1, one launch (start us, length us, event | category | flops | bytes accessed | tf_op | source)
XLA Modules:
  0.0 195.9 jit_solution(3177773548833800332)
XLA Ops:
  0.6 173.2 %shard_map.50 = (bf16[1024,4096]{1,0:T(8,128)(2,1)S(1)}, bf16[1024,512]{1,0:T(8,128)(2,1)S(1)}, f32[256,4096]{1,0:T(8,128)S(1)}, bf16[256,256]{1,0:T(8,128)(2,1)S(1)}) custom-call(bf16[1024,512]{1,0:T(8,128)(2,1)} %lower.1, bf16[1024,4096]{1,0:T(8,128)(2,1)} %side.1, bf16[1024,4096]{1,0:T(8,128)(2,1)} %grad.3), custom_call_target="tpu_custom_call" | custom-call | tf_op jit(solution)/shard_map/pallas_call | solution.py:409
  173.8 3.7 %shard_map.51 = (bf16[1024,4096]{1,0:T(8,128)(2,1)}, bf16[1024,512]{1,0:T(8,128)(2,1)}) custom-call(bf16[1024,4096]{1,0:T(8,128)(2,1)S(1)} %get-tuple-element.8.db_in, bf16[1024,512]{1,0:T(8,128)(2,1)S(1)} %get-tuple-element.9.dl_in), custom_call_target="tpu_custom_call" | custom-call | tf_op jit(solution)/shard_map/pallas_call | solution.py:442
  177.5 17.4 %shard_map.52.tail = bf16[256,1792]{1,0:T(8,128)(2,1)S(1)} custom-call(bf16[1024,4096]{1,0:T(8,128)(2,1)} %grad.3, f32[256,4096]{1,0:T(8,128)S(1)} %get-tuple-element.11.acc, bf16[256,256]{1,0:T(8,128)(2,1)S(1)} %get-tuple-element.12.weight, bf16[1024,512]{1,0:T(8,128)(2,1)} %get-tuple-element.7.dl), custom_call_target="tpu_custom_call" | custom-call | tf_op jit(solution)/shard_map/pallas_call | solution.py:451
  195.0 0.9 shard_map.53

commit v6 on v5

--- a/solution.py
+++ b/solution.py
@@ -10,6 +10,7 @@
 BF16 = jnp.bfloat16
 MESH = pl.DeviceIdType.MESH
 TILE = 256
+SHIFT = 64
 EARLY = ((0, 2304),)
 LATE = ((2304, 1536), (3840, 256),)
 CHUNKS = EARLY + LATE
@@ -66,21 +67,31 @@
     greet(second_core, across, next_chip)
     pl.when(first_core)(lambda: pl.semaphore_wait(barrier, 1))
 
-    near_src = (lower.at[pl.ds(BLK, 3 * BLK), pl.ds(0, BLK)], lower.at[pl.ds(3 * BLK, BLK), pl.ds(BLK, BLK)])
-    far_src = (lower.at[pl.ds(0, BLK), pl.ds(0, BLK)], lower.at[pl.ds(2 * BLK, BLK), pl.ds(BLK, BLK)])
-
-    def near_dst(q, h):
-        return wr.at[q, rows(1, 3)] if h == 0 else wr.at[q, rows(3)]
-
-    def far_dst(q):
-        return wr.at[q, rows(q)]
+    def low_rows(short):
+        return pl.ds(3 * BLK + SHIFT, BLK - SHIFT) if short else rows(3)
+
+    def near_src(h, short):
+        return lower.at[rows(1, 3), pl.ds(0, BLK)] if h == 0 else lower.at[low_rows(short), pl.ds(BLK, BLK)]
+
+    def near_dst(q, h, short=False):
+        return wr.at[q, rows(1, 3)] if h == 0 else wr.at[q, low_rows(short)]
+
+    far_rows = (rows(0), pl.ds(2 * BLK, BLK + SHIFT))
+    far_src = tuple(lower.at[far_rows[h], pl.ds(h * BLK, BLK)] for h in range(2))
+    far_via = (relay.at[0, pl.ds(0, BLK)], relay.at[1])
+
+    def far_dst(h):
+        return wr.at[2 * h, far_rows[h]]
+
+    far_sender = other & (r == 1) & (x == 0)
+    near_kinds = ((0, False, other, r >= 0), (1, False, other & jnp.logical_not(far_sender), (r == 1) | (x == 1)), (1, True, far_sender, (r == 0) & (x == 0)))
 
     def bulk(i, p):
         return copy_to(across, grad.at[rows(p)], xr.at[rows(p)], bulk_s.at[i], bulk_r.at[i])
 
     def first_copies(when):
-        for h in range(2):
-            start(when & other, copy_to(across, near_src[h], near_dst(x + 2 * h, h), near_s.at[h], near_r.at[x + 2 * h]))
+        for h, short, sends, _ in near_kinds:
+            start(when & sends, copy_to(across, near_src(h, short), near_dst(x + 2 * h, h, short), near_s.at[h], near_r.at[x + 2 * h]))
         start(when, bulk(0, 3))
 
     first_copies(first_core)
@@ -90,9 +101,8 @@
     greet(second_core, mate)
     pl.when(first_core)(lambda: pl.semaphore_wait(barrier, 1))
 
-    far_sender = other & (r == 1) & (x == 0)
     for h in range(2):
-        start(far_sender, copy_to(diagonal, far_src[h], relay.at[h], far_s.at[h], relay_r.at[h]))
+        start(far_sender, copy_to(diagonal, far_src[h], far_via[h], far_s.at[h], relay_r.at[h]))
 
     loads = [pltpu.make_async_copy(side.at[rows(q)], bl.at[rows(q)], load_s.at[q]) for q in range(4)]
     loads += [pltpu.make_async_copy(grad.at[rows(p)], xl.at[rows(p)], load_s.at[4 + p]) for p in range(4)]
@@ -139,24 +149,21 @@
 
     lax.fori_loop(0, 2 * NUM_LOCAL, local_outer, 0)
 
-    for h in range(2):
+    for h, short, _, receives in near_kinds:
         q = x + 2 * h
-
-        @pl.when(own)
-        def _():
-            arrived(near_dst(q, h), near_r.at[q])
-
+        there = near_dst(q, h, short)
+        pl.when(own & receives)(lambda: arrived(there, near_r.at[q]))
         for n, device in enumerate((mate, next_chip, diagonal)):
-            start(own, copy_to(device, near_dst(q, h), near_dst(q, h), near_s.at[2 + 3 * h + n], near_r.at[q]))
+            start(own & receives, copy_to(device, there, there, near_s.at[2 + 3 * h + n], near_r.at[q]))
     far_owner = other & (r == 0) & (x == 1)
     relay_here = own & (r == 1) & (x == 1)
     for h in range(2):
 
         @pl.when(relay_here)
         def _():
-            arrived(relay.at[h], relay_r.at[h])
-
-        start(relay_here, copy_to(across, relay.at[h], far_dst(2 * h), relay_s.at[h], far_r.at[h]))
+            arrived(far_via[h], relay_r.at[h])
+
+        start(relay_here, copy_to(across, far_via[h], far_dst(h), relay_s.at[h], far_r.at[h]))
     start(None, bulk(1, 2))
 
     def push(g):
@@ -237,12 +244,14 @@
     def weights_here(q):
         h = q // 2
         arrived(wl.at[q] if h == 0 else wl.at[q, rows(2, 2)], wl_r.at[q])
-        if h == 0:
-            pl.when(other | (x != q))(lambda: arrived(near_dst(q, h), near_r.at[q]))
+        elsewhere = other | (x + 2 * h != q)
+        if q == 2:
+            pl.when(elsewhere & (r == 0))(lambda: arrived(near_dst(q, h, True), near_r.at[q]))
+            pl.when(elsewhere & (r == 1))(lambda: arrived(near_dst(q, h), near_r.at[q]))
         else:
-            pl.when(other | (x + 2 != q))(lambda: arrived(near_dst(q, h), near_r.at[q]))
+            pl.when(elsewhere)(lambda: arrived(near_dst(q, h), near_r.at[q]))
         if q % 2 == 0:
-            pl.when((r == 0) & jnp.logical_not(far_owner))(lambda: arrived(far_dst(q), far_r.at[h]))
+            pl.when((r == 0) & jnp.logical_not(far_owner))(lambda: arrived(far_dst(h), far_r.at[h]))
 
     def block_row(q):
         weights_here(q)
@@ -274,10 +283,10 @@
 
         @pl.when(far_owner)
         def _():
-            arrived(far_dst(2 * h), far_r.at[h])
+            arrived(far_dst(h), far_r.at[h])
 
         for n, device in enumerate((mate, next_chip, diagonal)):
-            start(far_owner, copy_to(device, far_dst(2 * h), far_dst(2 * h), far_s.at[2 + 3 * h + n], far_r.at[h]))
+            start(far_owner, copy_to(device, far_dst(h), far_dst(h), far_s.at[2 + 3 * h + n], far_r.at[h]))
     push(1)
     add_and_cross(0)
     add_and_cross(1)
@@ -417,7 +426,7 @@
             pltpu.VMEM((num_rows, num_cols), BF16),
             pltpu.VMEM((4, 4 * BLK, BLK), BF16),
             pltpu.VMEM((4, 4 * BLK, BLK), BF16),
-            pltpu.VMEM((2, BLK, BLK), BF16),
+            pltpu.VMEM((2, BLK + SHIFT, BLK), BF16),
             pltpu.VMEM((NUM_SLOTS, 2, BLK, BLK), F32),
             pltpu.VMEM((NUM_SLOTS, 2, BLK, BLK), F32),
             pltpu.VMEM((NUM_SLOTS, BLK, BLK), F32),

time: 196 us -> 196 us (level)
  no operation moved by 1% of the time
where the time goes in v6:
time: 196 us
  Pallas kernels  195 us (99%)
    pallas_call x1, Pallas kernels, per_device(): pl.pallas_call(kernel, in_specs=[pl.BlockSpec(memory_space=pl.ANY)] * 3,...  173 us
    pallas_call x1, Pallas kernels, per_device(): pl.pallas_call(tail_kernel, in_specs=[in_hbm, in_vmem, in_vmem, in_hbm],...  17.1 us

profile of v6, /device:TPU:1, one launch (start us, length us, event | category | flops | bytes accessed | tf_op | source)
XLA Modules:
  0.0 195.6 jit_solution(733531731979536862)
XLA Ops:
  0.6 173.2 %shard_map.50 = (bf16[1024,4096]{1,0:T(8,128)(2,1)S(1)}, bf16[1024,512]{1,0:T(8,128)(2,1)S(1)}, f32[256,4096]{1,0:T(8,128)S(1)}, bf16[256,256]{1,0:T(8,128)(2,1)S(1)}) custom-call(bf16[1024,512]{1,0:T(8,128)(2,1)} %lower.1, bf16[1024,4096]{1,0:T(8,128)(2,1)} %side.1, bf16[1024,4096]{1,0:T(8,128)(2,1)} %grad.3), custom_call_target="tpu_custom_call" | custom-call | tf_op jit(solution)/shard_map/pallas_call | solution.py:418
  173.8 3.7 %shard_map.51 = (bf16[1024,4096]{1,0:T(8,128)(2,1)}, bf16[1024,512]{1,0:T(8,128)(2,1)}) custom-call(bf16[1024,4096]{1,0:T(8,128)(2,1)S(1)} %get-tuple-element.8.db_in, bf16[1024,512]{1,0:T(8,128)(2,1)S(1)} %get-tuple-element.9.dl_in), custom_call_target="tpu_custom_call" | custom-call | tf_op jit(solution)/shard_map/pallas_call | solution.py:451
  177.6 17.1 %shard_map.52.tail = bf16[256,1792]{1,0:T(8,128)(2,1)S(1)} custom-call(bf16[1024,4096]{1,0:T(8,128)(2,1)} %grad.3, f32[256,4096]{1,0:T(8,128)S(1)} %get-tuple-element.11.acc, bf16[256,256]{1,0:T(8,128)(2,1)S(1)} %get-tuple-element.12.weight, bf16[1024,512]{1,0:T(8,128)(2,1)} %get-tuple-element.7.dl), custom_call_target="tpu_custom_call" | custom-call | tf_op jit(solution)/shard_map/pallas_call | solution.py:460
  194.6 0.9 shard_map.53

commit v7 on v6

--- a/solution.py
+++ b/solution.py
@@ -457,23 +457,23 @@
         compiler_params=pltpu.CompilerParams(vmem_limit_bytes=1024 * 1024),
     )(keep(db), keep(dl))
     width = sum(w for _, w in LATE)
-    tail = pl.pallas_call(
+    tail, arrived = pl.pallas_call(
         tail_kernel,
         in_specs=[in_hbm, in_vmem, in_vmem, in_hbm],
-        out_specs=in_vmem,
-        out_shape=pltpu.VMEM((BLK, width), BF16),
-        scratch_shapes=[pltpu.VMEM((BLK, width), BF16), dma((len(LATE),)), dma((len(LATE),))],
+        out_specs=[in_vmem] * 2,
+        out_shape=[pltpu.VMEM((BLK, width), BF16)] * 2,
+        scratch_shapes=[dma((len(LATE),)), dma((len(LATE),))],
         compiler_params=pltpu.CompilerParams(collective_id=1, has_side_effects=True, vmem_limit_bytes=4 * 1024 * 1024),
     )(stay(grad), keep(acc), keep(weight), stay(dl))
     db = pl.pallas_call(
         put_tail_kernel,
-        in_specs=[anywhere, in_vmem],
+        in_specs=[anywhere] + [in_vmem] * 4,
         out_specs=anywhere,
         out_shape=jax.ShapeDtypeStruct(grad.shape, BF16),
         input_output_aliases={0: 0},
-        scratch_shapes=[dma],
-        compiler_params=pltpu.CompilerParams(vmem_limit_bytes=1024 * 1024),
-    )(db, keep(tail))
+        scratch_shapes=[pltpu.VMEM((BLK, LATE[-1][1]), BF16), dma((2,))],
+        compiler_params=pltpu.CompilerParams(vmem_limit_bytes=4 * 1024 * 1024),
+    )(db, keep(tail), keep(arrived), keep(acc), keep(weight))
     return db, dl
 
 
@@ -484,6 +484,10 @@
         copy.start()
     for copy in copies:
         copy.wait()
+
+
+def finished(weight, block, start_value):
+    return (start_value + lax.dot_general(weight, block, (((0,), (0,)), ((), ())), preferred_element_type=F32)).astype(BF16)
 
 
 def tail_kernel(grad, acc, weight, dl, tail, arriving, send_sem, recv_sem):
@@ -507,22 +511,28 @@
         @pl.when(receiver)
         def _():
             copies[i].wait_recv()
-            for n in range(width // TILE):
-                at = first - base + n * TILE
-                term = lax.dot_general(weight[...], arriving[:, pl.ds(at, TILE)], (((0,), (0,)), ((), ())), preferred_element_type=F32)
-                tail[:, pl.ds(at, TILE)] = (acc[:, pl.ds(base + at, TILE)] + term).astype(BF16)
+            if i < len(LATE) - 1:
+                for n in range(width // TILE):
+                    at = first - base + n * TILE
+                    tail[:, pl.ds(at, TILE)] = finished(weight[...], arriving[:, pl.ds(at, TILE)], acc[:, pl.ds(base + at, TILE)])
 
         pl.when(sender)(copies[i].wait_send)
 
 
-def put_tail_kernel(db_in, tail, db_out, sem):
+def put_tail_kernel(db_in, tail, arrived, acc, weight, db_out, last, sems):
     del db_in
+    base = LATE[0][0]
+    first, width = LATE[-1]
 
     @pl.when((lax.axis_index("row") == 0) & (lax.axis_index("col") % 2 == 1))
     def _():
-        copy = pltpu.make_async_copy(tail, db_out.at[rows(0), pl.ds(LATE[0][0], tail.shape[1])], sem)
-        copy.start()
-        copy.wait()
+        ready = pltpu.make_async_copy(tail.at[:, pl.ds(0, first - base)], db_out.at[rows(0), pl.ds(base, first - base)], sems.at[0])
+        ready.start()
+        last[...] = finished(weight[...], arrived[:, pl.ds(first - base, width)], acc[:, pl.ds(first, width)])
+        rest = pltpu.make_async_copy(last, db_out.at[rows(0), pl.ds(first, width)], sems.at[1])
+        rest.start()
+        ready.wait()
+        rest.wait()
 
 
 def solution(mesh):

time: 196 us -> 196 us (level)
  no operation moved by 1% of the time
where the time goes in v7:
time: 196 us; the launch traced here: 195 us
  Pallas kernels  195 us (99%)
    pallas_call x1, Pallas kernels, per_device(): pl.pallas_call(kernel, in_specs=[pl.BlockSpec(memory_space=pl.ANY)] * 3,...  173 us
    pallas_call x1, Pallas kernels, per_device(): pl.pallas_call(tail_kernel, in_specs=[in_hbm, in_vmem, in_vmem, in_hbm],...  16.8 us

profile of v7, /device:TPU:1, one launch (start us, length us, event | category | flops | bytes accessed | tf_op | source)
XLA Modules:
  0.0 195.4 jit_solution(8792468657658074631)
XLA Ops:
  0.6 173.2 %shard_map.50 = (bf16[1024,4096]{1,0:T(8,128)(2,1)S(1)}, bf16[1024,512]{1,0:T(8,128)(2,1)S(1)}, f32[256,4096]{1,0:T(8,128)S(1)}, bf16[256,256]{1,0:T(8,128)(2,1)S(1)}) custom-call(bf16[1024,512]{1,0:T(8,128)(2,1)} %lower.1, bf16[1024,4096]{1,0:T(8,128)(2,1)} %side.1, bf16[1024,4096]{1,0:T(8,128)(2,1)} %grad.3), custom_call_target="tpu_custom_call" | custom-call | tf_op jit(solution)/shard_map/pallas_call | solution.py:418
  173.8 3.7 %shard_map.51 = (bf16[1024,4096]{1,0:T(8,128)(2,1)}, bf16[1024,512]{1,0:T(8,128)(2,1)}) custom-call(bf16[1024,4096]{1,0:T(8,128)(2,1)S(1)} %get-tuple-element.10.db_in, bf16[1024,512]{1,0:T(8,128)(2,1)S(1)} %get-tuple-element.11.dl_in), custom_call_target="tpu_custom_call" | custom-call | tf_op jit(solution)/shard_map/pallas_call | solution.py:451
  177.6 16.8 %shard_map.52 = (bf16[256,1792]{1,0:T(8,128)(2,1)S(1)}, bf16[256,1792]{1,0:T(8,128)(2,1)S(1)}) custom-call(bf16[1024,4096]{1,0:T(8,128)(2,1)} %grad.3, f32[256,4096]{1,0:T(8,128)S(1)} %get-tuple-element.13.acc, bf16[256,256]{1,0:T(8,128)(2,1)S(1)} %get-tuple-element.14.weight, bf16[1024,512]{1,0:T(8,128)(2,1)} %get-tuple-element.9.dl), custom_call_target="tpu_custom_call" | custom-call | tf_op jit(solution)/shard_map/pallas_call | solution.py:460
  194.4 1.0 shard_map.53
